TPU v7x, 32 devices: a whole 2x2x4 slice. The times are simulated.
32 devices in a mesh: tok: 8 (over y, x, core), exp: 4 (over z).
Axes of the slice: x: 2, y: 2, z: 4, core: 2. Of those that a mesh axis runs over, the one named last changes fastest.
Arguments:
- expert_rows: bfloat16 [4, 2048, 4096], P('exp', 'tok'), may hold values from -480 to 480
- router_input: bfloat16 [2048, 4096], P(('tok', 'exp')), may hold values from -6 to 6
- router_weight: float32 [4096, 4], replicated, may hold values from -0.09375 to 0.09375
- assign: int32 [2048, 2], P(('tok', 'exp')), may hold values from 0 to 3, all different within a row
- targets: int32 [2048], P(('tok', 'exp')), may hold values from 0 to 15999
- head: bfloat16 [4096, 16000], P('tok', 'exp'), may hold values from -0.35 to 0.35
Outputs:
- token_loss: float32 [2048], P(('tok', 'exp'))
- router_grad: float32 [4096, 4], replicated
- mean_loss: float32 [], replicated
All inputs are finite; a program needn't handle non-finite values.
Results may differ from a plain program's by a relative error of at most 0.007.
Values may be sent and summed in bfloat16 or wider, within the bound.
A program may use at most 128 MiB of HBM per device.

v0:
```python
import math
import jax
import jax.numpy as jnp
from jax import lax
from jax.sharding import PartitionSpec as P


def shards(expert_rows, router_input, router_weight, assign, targets, head):
    experts = router_weight.shape[1]
    own_rows = router_input.shape[0]
    tokens_all = own_rows * lax.axis_size("tok") * lax.axis_size("exp")
    loss_scale = 1.0 / math.sqrt(tokens_all)
    inputs = router_input.astype(jnp.float32)
    gate_logits = jnp.dot(inputs, router_weight, precision=lax.Precision.HIGHEST)
    labels = jnp.arange(experts, dtype=jnp.int32)
    first_hot = (assign[:, 0:1] == labels[None, :]).astype(jnp.float32)
    second_hot = (assign[:, 1:2] == labels[None, :]).astype(jnp.float32)
    differ = first_hot - second_hot
    mix_share = jax.nn.sigmoid(jnp.sum(gate_logits * differ, axis=1))
    mixing = mix_share[:, None] * first_hot + (1.0 - mix_share)[:, None] * second_hot
    local_rows = lax.all_to_all(expert_rows, "exp", split_axis=1, concat_axis=0, tiled=True)
    local_wide = local_rows.astype(jnp.float32)
    mixed_own = jnp.sum(mixing.T[:, :, None] * local_wide, axis=0).astype(jnp.bfloat16)
    mixed_rows, group_targets = (
        lax.all_gather(mixed_own, "exp", axis=0, tiled=True),
        lax.all_gather(targets, "exp", axis=0, tiled=True),
    )
    shard_width = head.shape[1]
    full_head = lax.all_gather(head, "tok", axis=0, tiled=True)
    logits = jnp.dot(mixed_rows, full_head, preferred_element_type=jnp.float32)
    first_col = lax.axis_index("exp") * shard_width
    columns = first_col + jnp.arange(shard_width, dtype=jnp.int32)
    target_hit = group_targets[:, None] == columns[None, :]
    picked = jnp.sum(jnp.where(target_hit, logits, 0.0), axis=1)
    local_top = jnp.max(logits, axis=1)
    row_top = lax.pmax(local_top, "exp")
    exp_total, target_logit = lax.psum(
        (jnp.sum(jnp.exp(logits - row_top[:, None]), axis=1), picked), "exp"
    )
    log_total = row_top + jnp.log(exp_total)
    group_loss = log_total - target_logit
    own_loss = lax.dynamic_slice_in_dim(group_loss, lax.axis_index("exp") * own_rows, own_rows, 0)
    loss_sum = lax.psum(jnp.sum(own_loss), ("tok", "exp"))
    slope = (
        loss_scale * (jnp.exp(logits - log_total[:, None]) - target_hit.astype(jnp.float32))
    ).astype(jnp.bfloat16)
    hidden_slope = lax.psum_scatter(
        lax.dot_general(
            slope, full_head, (((1,), (1,)), ((), ())), preferred_element_type=jnp.float32
        ).astype(jnp.bfloat16),
        "exp",
        scatter_dimension=0,
        tiled=True,
    ).astype(jnp.float32)
    weight_slope = jnp.sum(hidden_slope[None, :, :] * local_wide, axis=2).T
    spread = jnp.sum(weight_slope * differ, axis=1) * mix_share * (1.0 - mix_share)
    gate_slope = spread[:, None] * differ
    router_part = jnp.dot(inputs.T, gate_slope, precision=lax.Precision.HIGHEST)
    router_sum = lax.psum(router_part, ("tok", "exp"))
    mean_loss = loss_sum / tokens_all
    return (own_loss, router_sum, mean_loss)


def solution(mesh):
    in_specs = (
        P("exp", "tok", None),
        P(("tok", "exp"), None),
        P(),
        P(("tok", "exp"), None),
        P(("tok", "exp")),
        P("tok", "exp"),
    )
    out_specs = (P(("tok", "exp")), P(), P())
    return jax.shard_map(shards, mesh=mesh, in_specs=in_specs, out_specs=out_specs, check_vma=False)
```

profile of v0, /device:TPU:1, one launch (start us, length us, event | category | flops | bytes accessed | tf_op | source)
XLA Modules:
  0.0 542.0 jit_solution(5459968139769704115)
XLA Ops:
  7.2 8.4 %copy.16 = bf16[1,256,4096]{2,0,1:T(2,128)(2,1)} copy(bf16[1,256,4096]{2,1,0:T(8,128)(2,1)} %param.6) | data formatting | bytes 4194304 | tf_op args[0]
  15.6 0.5 broadcast.107
  16.1 13.5 %reduce.1 = bf16[256,4096]{1,0:T(8,128)(2,1)S(1)} reduce(bf16[256,1,4096]{2,1,0:T(2,128)(2,1)} %bitcast.29, bf16[]{:T(256)} %broadcast.107), dimensions={1}, to_apply=%bitcast.25.reduce_sub_computation | reduce | bytes 4194306
  29.6 2.8 reshape.110
  32.4 5.4 all-to-all-start
  37.9 0.5 fusion.10
  38.4 47.2 %all-to-all-done = bf16[4,2,131072]{2,1,0:T(2,128)(2,1)S(1)} async-done(((bf16[4,2,131072]{2,1,0:T(2,128)(2,1)}), bf16[4,2,131072]{2,1,0:T(2,128)(2,1)S(1)}, u32[]{:S(2)}, u32[]{:S(2)}) %all-to-all-start) | async-done | bytes 2097184 | tf_op jit(solution)/shard_map/all_to_all | solution.py:21
  85.6 3.3 reshape.111
  88.9 6.0 %copy_convert_fusion = f32[1,256,4096]{2,1,0:T(8,128)S(1)} fusion(bf16[1,256,4096]{2,0,1:T(2,128)(2,1)} %bitcast.27), kind=kLoop, calls=%fused_computation.12 | loop fusion | flops 1048576 | bytes 6291456 | tf_op jit(solution)/shard_map/convert_element_type | solution.py:22
  94.9 1.4 multiply_reduce_fusion
  96.3 0.7 all-gather.5.cloned.1.call-update
  97.1 0.2 reduce-scatter.2.cloned.1.call-start
  97.3 0.6 dynamic-slice
  98.6 0.2 dynamic-update-slice
  98.8 4.0 all-reduce
  102.8 39.0 %all-gather.3.cloned.1.call-done = bf16[256,4096]{1,0:T(8,128)(2,1)} async-done(((bf16[64,4096]{1,0:T(8,128)(2,1)}), bf16[256,4096]{1,0:T(8,128)(2,1)}) %all-gather.3.cloned.1.call-update) | async-done | bytes 2097168 | tf_op jit(solution)/shard_map/all_gather | solution.py:25
  141.8 165.1 %all-gather.5.cloned.1.call-done = bf16[4096,4000]{0,1:T(8,128)(2,1)} async-done(((bf16[512,4000]{0,1:T(8,128)(2,1)}), bf16[4096,4000]{0,1:T(8,128)(2,1)}) %all-gather.5.cloned.1.call-update) | async-done | bytes 32768016 | tf_op jit(solution)/shard_map/all_gather | solution.py:29
  306.9 16.2 %fusion.19 = (f32[256]{0:T(256)S(1)}, f32[256,4000]{0,1:T(8,128)}) fusion(bf16[256,4096]{1,0:T(8,128)(2,1)} %all-gather.3.cloned.1.call-done, bf16[4096,4000]{0,1:T(8,128)(2,1)} %all-gather.5.cloned.1.call-done), kind=kOutput, calls=%fused_computation.41 | convolution fusion | flops 8389632000 | bytes 38962176 | tf_op jit(solution)/shard_map/dot_general | solution.py:30
  323.2 9.7 %pmax.7 = f32[256]{0:T(256)S(1)} all-reduce(f32[256]{0:T(256)S(1)} %get-tuple-element.15), channel_id=1, replica_groups=mesh['tok'=8,'exp'=4] {'exp'}, use_global_device_ids=true, to_apply=%region_3.4 | all-reduce | flops 256 | bytes 2048 | tf_op jit(solution)/shard_map/pmax | solution.py:36
  332.8 3.9 fusion.1
  336.7 6.6 %all-reduce.1 = (f32[256]{0:T(256)S(1)}, f32[256]{0:T(256)S(1)}) all-reduce(f32[256]{0:T(256)S(1)} %get-tuple-element.4, f32[256]{0:T(256)S(1)} %get-tuple-element.3), channel_id=1, replica_groups=mesh['tok'=8,'exp'=4] {'exp'}, use_global_device_ids=true, to_apply=%region_5.6 | all-reduce | flops 512 | bytes 4096 | tf_op jit(solution)/shard_map/psum | solution.py:37
  343.3 17.2 %convolution_convert_fusion = bf16[256,4096]{1,0:T(8,128)(2,1)} fusion(bf16[4096,4000]{0,1:T(8,128)(2,1)} %all-gather.5.cloned.1.call-done, f32[256,4000]{0,1:T(8,128)} %get-tuple-element.16, f32[256]{0:T(256)S(1)} %get-tuple-element.10, s32[256]{0:T(256)S(1)} %all-reduce, s32[4000]{0:T(1024)S(1)} %iota_add_fusion), kind=kOutput, calls=%fused_computation | convolution fusion | flops 8395800576 | bytes 38979200 | tf_op jit(solution)/shard_map/dot_general | solution.py:48
  360.6 45.4 %reduce-scatter.2.cloned.1.call-done = bf16[64,4096]{1,0:T(8,128)(2,1)} async-done(((bf16[256,4096]{1,0:T(8,128)(2,1)}), bf16[64,4096]{1,0:T(8,128)(2,1)}) %reduce-scatter.2.cloned.1.call-update) | async-done | bytes 524304 | tf_op jit(solution)/shard_map/reduce_scatter | solution.py:47
  406.0 1.7 mul.89
  407.6 0.7 copy-done.1
  408.3 2.4 fusion
  410.7 0.1 reduce_sum.70
  410.8 1.0 convolution_bitcast_fusion
  411.8 1.2 fusion.17
  413.0 39.8 %psum.31 = f32[]{:T(128)} all-reduce(f32[]{:T(128)} %get-tuple-element.7), channel_id=1, replica_groups=mesh['tok'=8,'exp'=4] {'tok','exp'}, use_global_device_ids=true, to_apply=%region_13.14 | all-reduce | flops 1 | bytes 8 | tf_op jit(solution)/shard_map/psum | solution.py:43
  453.4 79.5 %all-reduce.4.cloned.1.call-done = f32[4096,4]{0,1:T(4,128)} async-done(((f32[4096,4]{0,1:T(4,128)}), f32[4096,4]{0,1:T(4,128)}) %all-reduce.4.cloned.1.call-update) | async-done | bytes 65552 | tf_op jit(solution)/shard_map/psum | solution.py:59
  532.9 1.5 copy.19
  (25 shorter events, 0.2 us)
Async XLA Ops:
  7.2 30.7 %copy-start = (bf16[64,4096]{1,0:T(8,128)(2,1)S(1)}, bf16[64,4096]{1,0:T(8,128)(2,1)}, u32[]{:S(2)}) copy-start(bf16[64,4096]{1,0:T(8,128)(2,1)} %param.7) | copy-start | bytes 1572868
  29.6 8.2 %copy-start.3 = (s32[64,2]{0,1:T(2,128)S(1)}, s32[64,2]{0,1:T(2,128)}, u32[]{:S(2)}) copy-start(s32[64,2]{0,1:T(2,128)} %param.9) | copy-start | bytes 1540
  29.6 8.2 %copy-start.2 = (f32[4096,4]{0,1:T(4,128)S(1)}, f32[4096,4]{0,1:T(4,128)}, u32[]{:S(2)}) copy-start(f32[4096,4]{0,1:T(4,128)} %param.8) | copy-start | bytes 196612
  32.4 53.2 %all-to-all-start = ((bf16[4,2,131072]{2,1,0:T(2,128)(2,1)}), bf16[4,2,131072]{2,1,0:T(2,128)(2,1)S(1)}, u32[]{:S(2)}, u32[]{:S(2)}) async-start(bf16[4,2,131072]{2,1,0:T(2,128)(2,1)} %reshape.110), calls=%async_computation | async-start | bytes 4194304 | tf_op jit(solution)/shard_map/all_to_all | solution.py:21
  37.8 104.0 %all-gather.3.cloned.1.call-start = ((), (), s32[]{:S(2)}) async-start(), calls=%async_computation.2 | async-start | bytes 2621440 | tf_op jit(solution)/shard_map/all_gather | solution.py:25
  94.9 2.4 copy-start.5
  94.9 3.6 copy-start.4
  96.3 210.6 %all-gather.5.cloned.1.call-start = ((), (), s32[]{:S(2)}) async-start(), calls=%async_computation.3 | async-start | bytes 36864000 | tf_op jit(solution)/shard_map/all_gather | solution.py:29
  97.1 308.9 %reduce-scatter.2.cloned.1.call-start = ((), (), s32[]{:S(2)}) async-start(), calls=%async_computation.4 | async-start | bytes 2621440 | tf_op jit(solution)/shard_map/reduce_scatter | solution.py:47
  360.5 172.3 %all-reduce.4.cloned.1.call-start = ((), (), s32[]{:S(2)}) async-start(), calls=%async_computation.5 | async-start | bytes 131072 | tf_op jit(solution)/shard_map/psum | solution.py:59
  406.0 2.3 copy-start.1
Sparse Core Ops, SparseCore 0:
  96.4 45.3 all-gather.2
  143.6 163.2 all-gather.4
  360.7 45.2 reduce-scatter.1
  412.0 120.8 all-reduce.3
where the time goes:
time: 543 us; the launch traced here: 542 us
  waiting for transfers between devices  377 us (69%)
  blocking collectives  60.1 us (11%)
  matrix products  34.9 us (6%)
  other arithmetic  28.4 us (5%)
  local copies, waits for them, and re-layouts  19.7 us (4%)
  between operations  16.3 us (3%)
  starting transfers between devices  5.71 us (1%)
    all_gather x1, waiting for transfers between devices, shards(): full_head = lax.all_gather(head, 'tok', axis=0, tiled=True)  165 us
    psum x1, waiting for transfers between devices, shards(): router_sum = lax.psum(router_part, ('tok', 'exp'))  79.5 us
    all_to_all x1, waiting for transfers between devices, shards(): lax.all_to_all(expert_rows, 'exp', split_axis=1, concat_axis=0, tiled=True)  47.2 us
    reduce_scatter x1, waiting for transfers between devices, shards(): lax.psum_scatter(lax.dot_general(slope, full_head, (((1,), (1,)), ((), ()...  45.4 us
    psum x1, blocking collectives, shards(): loss_sum = lax.psum(jnp.sum(own_loss), ('tok', 'exp'))  39.8 us
    all_gather x1, waiting for transfers between devices, shards(): lax.all_gather(mixed_own, 'exp', axis=0, tiled=True)  39 us
    unnamed x20, local copies, waits for them, and re-layouts  18 us
    dot_general x1, matrix products, shards(): lax.dot_general(slope, full_head, (((1,), (1,)), ((), ())), preferred_ele...  17.2 us
  transfers between devices with their start and end apart: 5, of which 5 were waited for; matrix products, arithmetic and copies ran while one was open for 0% of the time, Pallas kernels for 0%

commit v1 on v0

--- a/solution.py
+++ b/solution.py
@@ -18,7 +18,12 @@
     differ = first_hot - second_hot
     mix_share = jax.nn.sigmoid(jnp.sum(gate_logits * differ, axis=1))
     mixing = mix_share[:, None] * first_hot + (1.0 - mix_share)[:, None] * second_hot
-    local_rows = lax.all_to_all(expert_rows, "exp", split_axis=1, concat_axis=0, tiled=True)
+    local_rows = jnp.concatenate(
+        lax.all_to_all(
+            jnp.stack(jnp.split(expert_rows, lax.axis_size("exp"), axis=1)), "exp", 0, 0
+        ),
+        axis=0,
+    )
     local_wide = local_rows.astype(jnp.float32)
     mixed_own = jnp.sum(mixing.T[:, :, None] * local_wide, axis=0).astype(jnp.bfloat16)
     mixed_rows, group_targets = (

time: 543 us -> 512 us (0.943)
  other arithmetic: 28.4 us -> 9.78 us
  local copies, waits for them, and re-layouts: 19.7 us -> 4.12 us
    unnamed x20 -> x14, local copies, waits for them, and re-layouts: 18 us -> 2.33 us
    unnamed x1 -> x0, other arithmetic: 13.5 us -> none
  transfers between devices with their start and end apart: 5 -> 5, of which waited for: 5 -> 5; matrix products, arithmetic and copies ran while one was open for 0% -> 1% of each run, Pallas kernels for 0% -> 0%
where the time goes in v1:
time: 512 us
  waiting for transfers between devices  381 us (74%)
  blocking collectives  59.7 us (12%)
  matrix products  35.5 us (7%)
  between operations  16.3 us (3%)
  other arithmetic  9.78 us (2%)
  starting transfers between devices  5.57 us (1%)
    all_gather x1, waiting for transfers between devices, shards(): full_head = lax.all_gather(head, 'tok', axis=0, tiled=True)  165 us
    psum x1, waiting for transfers between devices, shards(): router_sum = lax.psum(router_part, ('tok', 'exp'))  83 us
    all_to_all x1, waiting for transfers between devices, shards(): lax.all_to_all(jnp.stack(jnp.split(expert_rows, lax.axis_size('exp'), axi...  47.1 us
    reduce_scatter x1, waiting for transfers between devices, shards(): lax.psum_scatter(lax.dot_general(slope, full_head, (((1,), (1,)), ((), ()...  45.4 us
    psum x1, blocking collectives, shards(): loss_sum = lax.psum(jnp.sum(own_loss), ('tok', 'exp'))  39.4 us
    all_gather x1, waiting for transfers between devices, shards(): lax.all_gather(mixed_own, 'exp', axis=0, tiled=True)  39.1 us
    dot_general x1, matrix products, shards(): lax.dot_general(slope, full_head, (((1,), (1,)), ((), ())), preferred_ele...  17.2 us
    dot_general x1, matrix products, shards(): logits = jnp.dot(mixed_rows, full_head, preferred_element_type=jnp.float32)  16.9 us
  transfers between devices with their start and end apart: 5, of which 5 were waited for; matrix products, arithmetic and copies ran while one was open for 1% of the time, Pallas kernels for 0%

profile of v1, /device:TPU:1, one launch (start us, length us, event | category | flops | bytes accessed | tf_op | source)
XLA Modules:
  0.0 511.5 jit_solution(1747222428845513638)
XLA Ops:
  7.2 1.8 slice_bitcast_fusion.3
  9.0 1.6 pad_maximum_fusion
  10.6 5.4 %all-to-all-start = ((bf16[4,1,64,4096]{3,2,1,0:T(8,128)(2,1)}), bf16[4,1,64,4096]{3,2,1,0:T(8,128)(2,1)S(1)}, u32[]{:S(2)}, u32[]{:S(2)}) async-start(bf16[4,1,64,4096]{3,2,1,0:T(8,128)(2,1)} %pad_maximum_fusion), calls=%async_computation | async-start | bytes 4194304 | tf_op jit(solution)/shard_map/all_to_all | solution.py:22
  16.0 0.0 all-gather.3.cloned.1.call-start
  16.1 0.5 fusion.11
  16.7 47.1 %all-to-all-done = bf16[4,1,64,4096]{3,2,1,0:T(8,128)(2,1)S(1)} async-done(((bf16[4,1,64,4096]{3,2,1,0:T(8,128)(2,1)}), bf16[4,1,64,4096]{3,2,1,0:T(8,128)(2,1)S(1)}, u32[]{:S(2)}, u32[]{:S(2)}) %all-to-all-start) | async-done | bytes 2097184 | tf_op jit(solution)/shard_map/all_to_all | solution.py:22
  63.8 1.4 fusion
  65.2 0.0 all-gather.3.cloned.1.call-update
  65.2 0.0 all-gather.5.cloned.1.call-start
  65.2 0.7 all-gather.5.cloned.1.call-update
  65.9 0.0 reduce-scatter.2.cloned.1.call-start
  66.0 0.6 dynamic-slice
  67.3 0.2 dynamic-update-slice
  67.5 4.0 all-reduce
  71.5 39.1 %all-gather.3.cloned.1.call-done = bf16[256,4096]{1,0:T(8,128)(2,1)} async-done(((bf16[64,4096]{1,0:T(8,128)(2,1)}), bf16[256,4096]{1,0:T(8,128)(2,1)}) %all-gather.3.cloned.1.call-update) | async-done | bytes 2097168 | tf_op jit(solution)/shard_map/all_gather | solution.py:30
  110.7 165.1 %all-gather.5.cloned.1.call-done = bf16[4096,4000]{0,1:T(8,128)(2,1)} async-done(((bf16[512,4000]{0,1:T(8,128)(2,1)}), bf16[4096,4000]{0,1:T(8,128)(2,1)}) %all-gather.5.cloned.1.call-update) | async-done | bytes 32768016 | tf_op jit(solution)/shard_map/all_gather | solution.py:34
  275.8 16.9 %fusion.20 = (f32[256]{0:T(256)S(1)}, f32[256,4000]{0,1:T(8,128)}) fusion(bf16[256,4096]{1,0:T(8,128)(2,1)} %all-gather.3.cloned.1.call-done, bf16[4096,4000]{0,1:T(8,128)(2,1)} %all-gather.5.cloned.1.call-done), kind=kOutput, calls=%fused_computation.46 | convolution fusion | flops 8389632000 | bytes 38962176 | tf_op jit(solution)/shard_map/dot_general | solution.py:35
  292.7 9.6 %pmax.7 = f32[256]{0:T(256)S(1)} all-reduce(f32[256]{0:T(256)S(1)} %get-tuple-element.19), channel_id=1, replica_groups=mesh['tok'=8,'exp'=4] {'exp'}, use_global_device_ids=true, to_apply=%region_3.4 | all-reduce | flops 256 | bytes 2048 | tf_op jit(solution)/shard_map/pmax | solution.py:41
  302.3 3.9 fusion.2
  306.2 6.6 %all-reduce.1 = (f32[256]{0:T(256)S(1)}, f32[256]{0:T(256)S(1)}) all-reduce(f32[256]{0:T(256)S(1)} %get-tuple-element.4, f32[256]{0:T(256)S(1)} %get-tuple-element.3), channel_id=1, replica_groups=mesh['tok'=8,'exp'=4] {'exp'}, use_global_device_ids=true, to_apply=%region_5.6 | all-reduce | flops 512 | bytes 4096 | tf_op jit(solution)/shard_map/psum | solution.py:42
  312.8 17.2 %convolution_convert_fusion = bf16[256,4096]{1,0:T(8,128)(2,1)} fusion(bf16[4096,4000]{0,1:T(8,128)(2,1)} %all-gather.5.cloned.1.call-done, f32[256,4000]{0,1:T(8,128)} %get-tuple-element.20, f32[256]{0:T(256)S(1)} %get-tuple-element.10, s32[256]{0:T(256)S(1)} %all-reduce, s32[4000]{0:T(1024)S(1)} %iota_add_fusion), kind=kOutput, calls=%fused_computation.2 | convolution fusion | flops 8395800576 | bytes 38979200 | tf_op jit(solution)/shard_map/dot_general | solution.py:53
  330.0 0.0 reduce-scatter.2.cloned.1.call-update
  330.0 0.0 all-reduce.4.cloned.1.call-start
  330.1 45.4 %reduce-scatter.2.cloned.1.call-done = bf16[64,4096]{1,0:T(8,128)(2,1)} async-done(((bf16[256,4096]{1,0:T(8,128)(2,1)}), bf16[64,4096]{1,0:T(8,128)(2,1)}) %reduce-scatter.2.cloned.1.call-update) | async-done | bytes 524304 | tf_op jit(solution)/shard_map/reduce_scatter | solution.py:52
  375.4 1.1 convert_element_type.36
  376.5 0.5 fusion.1
  377.1 1.0 convolution_bitcast_fusion
  378.1 0.0 all-reduce.4.cloned.1.call-update
  378.1 1.2 fusion.18
  379.3 39.4 %psum.31 = f32[]{:T(128)} all-reduce(f32[]{:T(128)} %get-tuple-element.7), channel_id=1, replica_groups=mesh['tok'=8,'exp'=4] {'tok','exp'}, use_global_device_ids=true, to_apply=%region_13.14 | all-reduce | flops 1 | bytes 8 | tf_op jit(solution)/shard_map/psum | solution.py:48
  419.3 83.0 %all-reduce.4.cloned.1.call-done = f32[4096,4]{0,1:T(4,128)} async-done(((f32[4096,4]{0,1:T(4,128)}), f32[4096,4]{0,1:T(4,128)}) %all-reduce.4.cloned.1.call-update) | async-done | bytes 65552 | tf_op jit(solution)/shard_map/psum | solution.py:64
  502.4 1.5 copy.11
  (18 shorter events, 0.1 us)
Async XLA Ops:
  7.2 8.9 %copy-start = (bf16[64,4096]{1,0:T(8,128)(2,1)S(1)}, bf16[64,4096]{1,0:T(8,128)(2,1)}, u32[]{:S(2)}) copy-start(bf16[64,4096]{1,0:T(8,128)(2,1)} %param.7) | copy-start | bytes 1572868
  9.0 7.1 %copy-start.2 = (s32[64,2]{0,1:T(2,128)S(1)}, s32[64,2]{0,1:T(2,128)}, u32[]{:S(2)}) copy-start(s32[64,2]{0,1:T(2,128)} %param.9) | copy-start | bytes 1540
  9.0 7.1 %copy-start.1 = (f32[4096,4]{0,1:T(4,128)S(1)}, f32[4096,4]{0,1:T(4,128)}, u32[]{:S(2)}) copy-start(f32[4096,4]{0,1:T(4,128)} %param.8) | copy-start | bytes 196612
  10.6 53.2 %all-to-all-start = ((bf16[4,1,64,4096]{3,2,1,0:T(8,128)(2,1)}), bf16[4,1,64,4096]{3,2,1,0:T(8,128)(2,1)S(1)}, u32[]{:S(2)}, u32[]{:S(2)}) async-start(bf16[4,1,64,4096]{3,2,1,0:T(8,128)(2,1)} %pad_maximum_fusion), calls=%async_computation | async-start | bytes 4194304 | tf_op jit(solution)/shard_map/all_to_all | solution.py:22
  16.0 50.0 %copy-start.4 = (u32[32]{0:T(128)S(1)}, u32[32]{0:T(128)}, u32[]{:S(2)}) copy-start(u32[32]{0:T(128)} %constant.28) | copy-start | bytes 388
  16.0 51.2 %copy-start.3 = (s32[64]{0:T(128)S(1)}, s32[64]{0:T(128)}, u32[]{:S(2)}) copy-start(s32[64]{0:T(128)} %param.10) | copy-start | bytes 772
  16.0 94.6 %all-gather.3.cloned.1.call-start = ((), (), s32[]{:S(2)}) async-start(), calls=%async_computation.2 | async-start | bytes 2621440 | tf_op jit(solution)/shard_map/all_gather | solution.py:30
  65.2 210.6 %all-gather.5.cloned.1.call-start = ((), (), s32[]{:S(2)}) async-start(), calls=%async_computation.3 | async-start | bytes 36864000 | tf_op jit(solution)/shard_map/all_gather | solution.py:34
  65.9 309.5 %reduce-scatter.2.cloned.1.call-start = ((), (), s32[]{:S(2)}) async-start(), calls=%async_computation.4 | async-start | bytes 2621440 | tf_op jit(solution)/shard_map/reduce_scatter | solution.py:52
  330.0 172.4 %all-reduce.4.cloned.1.call-start = ((), (), s32[]{:S(2)}) async-start(), calls=%async_computation.5 | async-start | bytes 131072 | tf_op jit(solution)/shard_map/psum | solution.py:64
Sparse Core Ops, SparseCore 0:
  65.3 45.3 all-gather.2
  112.5 163.2 all-gather.4
  330.1 45.2 reduce-scatter.1
  381.4 120.8 all-reduce.3
